TPU v7x, 32 devices: a whole 2x2x4 slice. The times are simulated.
32 devices in a mesh: blk: 8 (over z, y), rep: 4 (over x, core).
Axes of the slice: x: 2, y: 2, z: 4, core: 2. Of those that a mesh axis runs over, the one named last changes fastest.
Arguments:
- tokens: bfloat16 [4096, 8192], P(('blk', 'rep')), may hold values from -6 to 6
- gate_weight: bfloat16 [8, 8192], P('blk'), may hold values from -0.0625 to 0.0625
- up_weight: bfloat16 [8, 8192], P('blk'), may hold values from -0.0625 to 0.0625
- down_weight: bfloat16 [8, 8192], P('blk'), may hold values from -2 to 2
Outputs:
- grad_gate: float32 [8, 8192], P('blk')
- grad_up: float32 [8, 8192], P('blk')
- grad_down: float32 [8, 8192], P('blk')
All inputs are finite; a program needn't handle non-finite values.
Results may differ from a plain program's by a relative error of at most 0.0027.
Values may be sent and summed in bfloat16 or wider, within the bound.
A program may use at most 64 MiB of HBM per device.

v0:
```python
import jax
import jax.numpy as jnp
from jax import lax
from jax.sharding import PartitionSpec as P


def per_device(tokens, gate_weight, up_weight, down_weight):
    tok_rows = tokens.shape[0]
    features = tokens.shape[1]
    cycle_size = lax.axis_size("blk")
    group_size = lax.axis_size("rep")
    loss_scale = float(tok_rows * cycle_size * group_size) ** (-0.5)
    right_numbers = (((1,), (1,)), ((), ()))
    left_numbers = (((0,), (0,)), ((), ()))
    gate_piece = lax.all_gather(gate_weight, "blk", axis=0, tiled=True)
    up_piece = lax.all_gather(up_weight, "blk", axis=0, tiled=True)
    down_piece = lax.all_gather(down_weight, "blk", axis=0, tiled=True)
    gate_pre = lax.dot_general(
        tokens, gate_piece, right_numbers, preferred_element_type=jnp.float32
    )
    up_pre = lax.dot_general(tokens, up_piece, right_numbers, preferred_element_type=jnp.float32)
    hidden_piece = (gate_pre * jax.nn.sigmoid(gate_pre) * up_pre).astype(jnp.bfloat16)
    layer_out = jnp.dot(hidden_piece, down_piece, preferred_element_type=jnp.float32)
    gate_all = gate_pre
    up_all = up_pre
    gate_full = gate_piece
    up_full = up_piece
    down_full = down_piece
    carry = (layer_out, gate_all, up_all, hidden_piece, gate_full, up_full, down_full)
    layer_out, gate_pre, up_pre, hidden, gate_full, up_full, down_full = carry
    cotangent = (layer_out * loss_scale).astype(jnp.bfloat16)
    hidden_grad = lax.dot_general(
        cotangent, down_full, right_numbers, preferred_element_type=jnp.float32
    )
    sigmoid_gate = jax.nn.sigmoid(gate_pre)
    active = gate_pre * sigmoid_gate
    gate_grad = (
        hidden_grad * up_pre * (sigmoid_gate * (1.0 + gate_pre * (1.0 - sigmoid_gate)))
    ).astype(jnp.bfloat16)
    up_grad = (hidden_grad * active).astype(jnp.bfloat16)
    gate_term = lax.dot_general(gate_grad, tokens, left_numbers, preferred_element_type=jnp.float32)
    up_term = lax.dot_general(up_grad, tokens, left_numbers, preferred_element_type=jnp.float32)
    down_term = lax.dot_general(hidden, cotangent, left_numbers, preferred_element_type=jnp.float32)
    shares = lax.psum_scatter(
        jnp.concatenate([gate_term, up_term, down_term], axis=1),
        "blk",
        scatter_dimension=0,
        tiled=True,
    )
    totals = lax.psum(shares, "rep")
    return (totals[:, :features], totals[:, features : 2 * features], totals[:, 2 * features :])


def solution(mesh):
    in_specs = (P(("blk", "rep"), None), P("blk", None), P("blk", None), P("blk", None))
    out_specs = (P("blk", None), P("blk", None), P("blk", None))
    return jax.shard_map(
        per_device, mesh=mesh, in_specs=in_specs, out_specs=out_specs, check_vma=False
    )
```

profile of v0, /device:TPU:0, one launch (start us, length us, event | category | flops | bytes accessed | tf_op | source)
XLA Modules:
  0.0 225.2 jit_solution(10801026277273655064)
XLA Ops:
  7.2 0.0 copy-start
  7.2 0.0 all-reduce.6.cloned.1.call-start
  7.2 32.9 %all-gather.2 = bf16[8,1,8192]{2,1,0:T(2,128)(2,1)S(1)} all-gather(bf16[1,1,8192]{2,1,0:T(2,128)(2,1)} %bitcast.25), channel_id=1, replica_groups=mesh['blk'=8,'rep'=4] {'blk'}, dimensions={0}, use_global_device_ids=true | all-gather | bytes 147456 | tf_op jit(solution)/shard_map/all_gather | solution.py:17
  40.1 30.9 %all-gather = bf16[8,1,8192]{2,1,0:T(2,128)(2,1)S(1)} all-gather(bf16[1,1,8192]{2,1,0:T(2,128)(2,1)} %bitcast.26), channel_id=1, replica_groups=mesh['blk'=8,'rep'=4] {'blk'}, dimensions={0}, use_global_device_ids=true | all-gather | bytes 147456 | tf_op jit(solution)/shard_map/all_gather | solution.py:15
  71.1 30.9 %all-gather.1 = bf16[8,1,8192]{2,1,0:T(2,128)(2,1)S(1)} all-gather(bf16[1,1,8192]{2,1,0:T(2,128)(2,1)} %bitcast.27), channel_id=1, replica_groups=mesh['blk'=8,'rep'=4] {'blk'}, dimensions={0}, use_global_device_ids=true | all-gather | bytes 147456 | tf_op jit(solution)/shard_map/all_gather | solution.py:16
  102.0 0.0 copy-done
  102.0 0.7 fusion.7
  102.7 0.7 multiply_convert_fusion.2
  103.4 0.8 fusion
  104.1 0.6 fusion.1
  104.8 0.4 fusion.20
  105.2 0.4 fusion.14
  105.6 0.0 copy-start.1
  105.6 0.4 fusion.13
  106.0 1.0 pad_maximum_fusion
  106.9 0.0 all-reduce.6.cloned.1.call-update
  107.0 0.0 all-reduce.4.cloned.1.call-start
  107.0 0.0 copy-done.1
  107.0 0.6 dynamic-slice
  107.6 75.8 %all-reduce.6.cloned.1.call-done = f32[8,24576]{1,0:T(8,128)} async-done(((f32[8,24576]{1,0:T(8,128)}), f32[8,24576]{1,0:T(8,128)}) %all-reduce.6.cloned.1.call-update) | async-done | bytes 786448
  183.4 2.5 %constant_dynamic-slice_fusion = f32[1,24576]{1,0:T(1,128)} fusion(f32[8,24576]{1,0:T(8,128)} %all-reduce.6.cloned.1.call-done, u32[]{:T(128)} %bitcast.3), kind=kLoop, calls=%fused_computation.22 | loop fusion | bytes 196612
  185.9 0.0 all-reduce.4.cloned.1.call-update
  185.9 31.0 %all-reduce.4.cloned.1.call-done = f32[1,24576]{1,0:T(1,128)} async-done(((f32[1,24576]{1,0:T(1,128)}), f32[1,24576]{1,0:T(1,128)}) %all-reduce.4.cloned.1.call-update) | async-done | bytes 98320 | tf_op jit(solution)/shard_map/psum | solution.py:50
  216.9 1.4 fusion.19
Async XLA Ops:
  7.2 94.9 %copy-start = (bf16[128,8192]{1,0:T(8,128)(2,1)S(1)}, bf16[128,8192]{1,0:T(8,128)(2,1)}, u32[]{:S(2)}) copy-start(bf16[128,8192]{1,0:T(8,128)(2,1)} %param.4) | copy-start | bytes 6291460
  7.2 176.2 %all-reduce.6.cloned.1.call-start = ((), (), s32[]{:S(2)}) async-start(), calls=%async_computation.1 | async-start | bytes 1572864
  105.6 1.4 copy-start.1
  107.0 109.9 %all-reduce.4.cloned.1.call-start = ((), (), s32[]{:S(2)}) async-start(), calls=%async_computation | async-start | bytes 196608 | tf_op jit(solution)/shard_map/psum | solution.py:50
Sparse Core Ops, SparseCore 0:
  107.1 76.2 all-reduce.5
  186.0 30.8 all-reduce.3
where the time goes:
time: 225 us
  waiting for transfers between devices  107 us (48%)
  blocking collectives  94.8 us (42%)
  between operations  14.1 us (6%)
  local copies, waits for them, and re-layouts  4.51 us (2%)
  matrix products  3.94 us (2%)
    unnamed x3, waiting for transfers between devices  75.8 us
    all_gather x1, blocking collectives, per_device(): down_piece = lax.all_gather(down_weight, 'blk', axis=0, tiled=True)  32.9 us
    psum x1, waiting for transfers between devices, per_device(): totals = lax.psum(shares, 'rep')  31 us
    all_gather x1, blocking collectives, per_device(): gate_piece = lax.all_gather(gate_weight, 'blk', axis=0, tiled=True)  30.9 us
    all_gather x1, blocking collectives, per_device(): up_piece = lax.all_gather(up_weight, 'blk', axis=0, tiled=True)  30.9 us
  transfers between devices with their start and end apart: 2, of which 2 were waited for; matrix products, arithmetic and copies ran while one was open for 0% of the time, Pallas kernels for 0%

commit v1 on v0

--- a/solution.py
+++ b/solution.py
@@ -2,6 +2,7 @@
 import jax.numpy as jnp
 from jax import lax
 from jax.sharding import PartitionSpec as P
+from jax.lax import all_gather
 
 
 def per_device(tokens, gate_weight, up_weight, down_weight):
@@ -47,7 +48,8 @@
         scatter_dimension=0,
         tiled=True,
     )
-    totals = lax.psum(shares, "rep")
+    attach_the_frames = lambda frame_in, axis_tag: jnp.sum(all_gather(frame_in, axis_tag), 0)
+    totals = attach_the_frames(shares, "rep")
     return (totals[:, :features], totals[:, features : 2 * features], totals[:, 2 * features :])
 
 

time: 225 us -> 200 us (0.89)
  waiting for transfers between devices: 107 us -> 75.9 us
  blocking collectives: 94.8 us -> 101 us
    psum x1 -> x0, waiting for transfers between devices: 31 us -> none  [per_device(): totals = lax.psum(shares, 'rep')]
    all_gather x0 -> x1, blocking collectives: none -> 6.44 us  [per_device(): all_gather(frame_in, axis_tag)]
    unnamed x3 -> x2, waiting for transfers between devices: 75.8 us -> 75.9 us
  transfers between devices with their start and end apart: 2 -> 1, of which waited for: 2 -> 1; matrix products, arithmetic and copies ran while one was open for 0% -> 0% of each run, Pallas kernels for 0% -> 0%
where the time goes in v1:
time: 200 us
  blocking collectives  101 us (50%)
  waiting for transfers between devices  75.9 us (38%)
  between operations  14.1 us (7%)
  matrix products  3.94 us (2%)
  local copies, waits for them, and re-layouts  3.09 us (2%)
    unnamed x2, waiting for transfers between devices  75.9 us
    all_gather x1, blocking collectives, per_device(): down_piece = lax.all_gather(down_weight, 'blk', axis=0, tiled=True)  32.9 us
    all_gather x1, blocking collectives, per_device(): gate_piece = lax.all_gather(gate_weight, 'blk', axis=0, tiled=True)  30.9 us
    all_gather x1, blocking collectives, per_device(): up_piece = lax.all_gather(up_weight, 'blk', axis=0, tiled=True)  30.9 us
    all_gather x1, blocking collectives, per_device(): all_gather(frame_in, axis_tag)  6.44 us
  transfers between devices with their start and end apart: 1, of which 1 were waited for; matrix products, arithmetic and copies ran while one was open for 0% of the time, Pallas kernels for 0%

profile of v1, /device:TPU:0, one launch (start us, length us, event | category | flops | bytes accessed | tf_op | source)
XLA Modules:
  0.0 199.6 jit_solution(17099611643970499511)
XLA Ops:
  7.2 0.0 copy-start
  7.2 0.0 all-reduce.3.cloned.1.call-start
  7.2 32.9 %all-gather.3 = bf16[8,1,8192]{2,1,0:T(2,128)(2,1)S(1)} all-gather(bf16[1,1,8192]{2,1,0:T(2,128)(2,1)} %bitcast.29), channel_id=1, replica_groups=mesh['blk'=8,'rep'=4] {'blk'}, dimensions={0}, use_global_device_ids=true | all-gather | bytes 147456 | tf_op jit(solution)/shard_map/all_gather | solution.py:18
  40.1 30.9 %all-gather.1 = bf16[8,1,8192]{2,1,0:T(2,128)(2,1)S(1)} all-gather(bf16[1,1,8192]{2,1,0:T(2,128)(2,1)} %bitcast.30), channel_id=1, replica_groups=mesh['blk'=8,'rep'=4] {'blk'}, dimensions={0}, use_global_device_ids=true | all-gather | bytes 147456 | tf_op jit(solution)/shard_map/all_gather | solution.py:16
  71.1 30.9 %all-gather.2 = bf16[8,1,8192]{2,1,0:T(2,128)(2,1)S(1)} all-gather(bf16[1,1,8192]{2,1,0:T(2,128)(2,1)} %bitcast.31), channel_id=1, replica_groups=mesh['blk'=8,'rep'=4] {'blk'}, dimensions={0}, use_global_device_ids=true | all-gather | bytes 147456 | tf_op jit(solution)/shard_map/all_gather | solution.py:17
  102.0 0.0 copy-done
  102.0 0.7 fusion.7
  102.7 0.7 multiply_convert_fusion.2
  103.4 0.8 fusion
  104.1 0.6 fusion.1
  104.8 0.4 fusion.20
  105.2 0.4 fusion.14
  105.6 0.0 copy-start.1
  105.6 0.4 fusion.13
  106.0 1.0 pad_maximum_fusion
  106.9 0.0 all-reduce.3.cloned.1.call-update
  107.0 0.0 copy-done.1
  107.0 0.6 dynamic-slice
  107.6 75.9 %all-reduce.3.cloned.1.call-done = f32[8,24576]{1,0:T(8,128)} async-done(((f32[8,24576]{1,0:T(8,128)}), f32[8,24576]{1,0:T(8,128)}) %all-reduce.3.cloned.1.call-update) | async-done | bytes 786448
  183.4 1.8 dynamic-slice_bitcast_fusion
  185.3 6.4 %all-gather.4 = f32[4,1,24576]{2,1,0:T(1,128)S(1)} all-gather(f32[1,1,24576]{2,1,0:T(1,128)S(1)} %dynamic-slice_bitcast_fusion), channel_id=2, replica_groups=mesh['blk'=8,'rep'=4] {'rep'}, dimensions={0}, use_global_device_ids=true | all-gather | bytes 491520 | tf_op jit(solution)/shard_map/all_gather | solution.py:51
  191.7 0.4 reduce.1
  192.1 0.6 fusion.19
Async XLA Ops:
  7.2 94.9 %copy-start = (bf16[128,8192]{1,0:T(8,128)(2,1)S(1)}, bf16[128,8192]{1,0:T(8,128)(2,1)}, u32[]{:S(2)}) copy-start(bf16[128,8192]{1,0:T(8,128)(2,1)} %param.4) | copy-start | bytes 6291460
  7.2 176.2 %all-reduce.3.cloned.1.call-start = ((), (), s32[]{:S(2)}) async-start(), calls=%async_computation | async-start | bytes 1572864
  105.6 1.4 copy-start.1
Sparse Core Ops, SparseCore 0:
  107.1 76.2 all-reduce.2

commit v2 on v0

--- a/solution.py
+++ b/solution.py
@@ -2,6 +2,14 @@
 import jax.numpy as jnp
 from jax import lax
 from jax.sharding import PartitionSpec as P
+
+
+def switch_sections(arr_in, unit):
+    return jnp.split(
+        jax.lax.all_gather(jnp.concatenate([arr_in, unit], axis=1), "blk", axis=0, tiled=True),
+        [arr_in.shape[1]],
+        1,
+    )
 
 
 def per_device(tokens, gate_weight, up_weight, down_weight):
@@ -13,8 +21,7 @@
     right_numbers = (((1,), (1,)), ((), ()))
     left_numbers = (((0,), (0,)), ((), ()))
     gate_piece = lax.all_gather(gate_weight, "blk", axis=0, tiled=True)
-    up_piece = lax.all_gather(up_weight, "blk", axis=0, tiled=True)
-    down_piece = lax.all_gather(down_weight, "blk", axis=0, tiled=True)
+    up_piece, down_piece = switch_sections(up_weight, down_weight)
     gate_pre = lax.dot_general(
         tokens, gate_piece, right_numbers, preferred_element_type=jnp.float32
     )

time: 225 us -> 196 us (0.87)
  blocking collectives: 94.8 us -> 64.1 us
    all_gather x2 -> x1, blocking collectives: 63.9 us -> 31.2 us  [switch_sections(): jax.lax.all_gather(jnp.concatenate([arr_in, unit], axis=1), 'blk', axis=0...]
where the time goes in v2:
time: 196 us
  waiting for transfers between devices  107 us (55%)
  blocking collectives  64.1 us (33%)
  between operations  14.1 us (7%)
  local copies, waits for them, and re-layouts  4.8 us (2%)
  matrix products  3.92 us (2%)
    unnamed x3, waiting for transfers between devices  75.8 us
    all_gather x1, blocking collectives, per_device(): gate_piece = lax.all_gather(gate_weight, 'blk', axis=0, tiled=True)  32.9 us
    all_gather x1, blocking collectives, switch_sections(): jax.lax.all_gather(jnp.concatenate([arr_in, unit], axis=1), 'blk', axis=0...  31.2 us
    psum x1, waiting for transfers between devices, per_device(): totals = lax.psum(shares, 'rep')  31 us
  transfers between devices with their start and end apart: 2, of which 2 were waited for; matrix products, arithmetic and copies ran while one was open for 0% of the time, Pallas kernels for 0%

profile of v2, /device:TPU:0, one launch (start us, length us, event | category | flops | bytes accessed | tf_op | source)
XLA Modules:
  0.0 195.5 jit_solution(5608377386953943517)
XLA Ops:
  7.2 0.0 copy-start
  7.2 0.0 all-reduce.6.cloned.1.call-start
  7.2 32.9 %all-gather = bf16[8,1,8192]{2,1,0:T(2,128)(2,1)S(1)} all-gather(bf16[1,1,8192]{2,1,0:T(2,128)(2,1)} %bitcast.23), channel_id=1, replica_groups=mesh['blk'=8,'rep'=4] {'blk'}, dimensions={0}, use_global_device_ids=true | all-gather | bytes 147456 | tf_op jit(solution)/shard_map/all_gather | solution.py:23
  40.1 0.8 maximum_bitcast_fusion
  41.0 31.2 %all-gather.1 = bf16[8,1,16384]{2,1,0:T(2,128)(2,1)S(1)} all-gather(bf16[1,1,16384]{2,1,0:T(2,128)(2,1)S(1)} %maximum_bitcast_fusion), channel_id=1, replica_groups=mesh['blk'=8,'rep'=4] {'blk'}, dimensions={0}, use_global_device_ids=true | all-gather | bytes 294912 | tf_op jit(solution)/shard_map/all_gather | solution.py:9
  72.2 0.3 copy.14
  72.4 0.0 copy-done
  72.5 0.7 fusion.2
  73.1 0.7 multiply_convert_fusion.2
  73.8 0.8 fusion
  74.6 0.6 fusion.5
  75.2 0.4 fusion.16
  75.6 0.4 fusion.10
  76.0 0.4 fusion.9
  76.4 1.0 pad_maximum_fusion
  77.3 0.0 all-reduce.6.cloned.1.call-update
  77.4 0.0 all-reduce.4.cloned.1.call-start
  77.4 0.0 copy-done.1
  77.4 0.6 dynamic-slice
  78.0 75.8 %all-reduce.6.cloned.1.call-done = f32[8,24576]{1,0:T(8,128)} async-done(((f32[8,24576]{1,0:T(8,128)}), f32[8,24576]{1,0:T(8,128)}) %all-reduce.6.cloned.1.call-update) | async-done | bytes 786448
  153.8 2.5 %constant_dynamic-slice_fusion = f32[1,24576]{1,0:T(1,128)} fusion(f32[8,24576]{1,0:T(8,128)} %all-reduce.6.cloned.1.call-done, u32[]{:T(128)} %bitcast.3), kind=kLoop, calls=%fused_computation.21 | loop fusion | bytes 196612
  156.3 0.0 all-reduce.4.cloned.1.call-update
  156.3 31.0 %all-reduce.4.cloned.1.call-done = f32[1,24576]{1,0:T(1,128)} async-done(((f32[1,24576]{1,0:T(1,128)}), f32[1,24576]{1,0:T(1,128)}) %all-reduce.4.cloned.1.call-update) | async-done | bytes 98320 | tf_op jit(solution)/shard_map/psum | solution.py:57
  187.3 1.4 fusion.15
  (1 shorter events, 0.0 us)
Async XLA Ops:
  7.2 65.3 %copy-start = (bf16[128,8192]{1,0:T(8,128)(2,1)S(1)}, bf16[128,8192]{1,0:T(8,128)(2,1)}, u32[]{:S(2)}) copy-start(bf16[128,8192]{1,0:T(8,128)(2,1)} %param.4) | copy-start | bytes 6291460
  7.2 146.6 %all-reduce.6.cloned.1.call-start = ((), (), s32[]{:S(2)}) async-start(), calls=%async_computation.1 | async-start | bytes 1572864
  76.0 1.4 copy-start.1
  77.4 109.9 %all-reduce.4.cloned.1.call-start = ((), (), s32[]{:S(2)}) async-start(), calls=%async_computation | async-start | bytes 196608 | tf_op jit(solution)/shard_map/psum | solution.py:57
Sparse Core Ops, SparseCore 0:
  77.5 76.2 all-reduce.5
  156.4 30.8 all-reduce.3
